TPU v7x, 256 devices: a whole 4x4x8 slice. The times are simulated.
256 devices in a mesh: fsdp: 16 (over y, x), width: 16 (over z, core).
Axes of the slice: x: 4, y: 4, z: 8, core: 2. Of those that a mesh axis runs over, the one named last changes fastest.
Arguments:
- train_gate: float32 [4096, 11008], P('fsdp', 'width'), may hold values from -0.125 to 0.125
- drift_gate: float32 [4096, 11008], P('fsdp', 'width'), may hold values from -0.09375 to 0.09375
- spread_gate: float32 [4096, 11008], P('fsdp', 'width'), may hold values from -0.09375 to 0.09375
- train_up: float32 [4096, 11008], P('fsdp', 'width'), may hold values from -0.125 to 0.125
- drift_up: float32 [4096, 11008], P('fsdp', 'width'), may hold values from -0.09375 to 0.09375
- spread_up: float32 [4096, 11008], P('fsdp', 'width'), may hold values from -0.09375 to 0.09375
- norm_train: float32 [4096], P(('fsdp', 'width')), may hold values from 0.25 to 1.75
- norm_step: float32 [4096], P(('fsdp', 'width')), may hold values from -0.3 to 0.3
Outputs:
- serving_gate: bfloat16 [4096, 11008], P(None, 'width')
- serving_up: bfloat16 [4096, 11008], P(None, 'width')
- scale_gate: float32 [11008], P('width')
- scale_up: float32 [11008], P('width')
- serve_norm: bfloat16 [4096], replicated
- whole_gate: float32 [4096, 11008], P('fsdp', 'width')
- whole_up: float32 [4096, 11008], P('fsdp', 'width')
All inputs are finite; a program needn't handle non-finite values.
Results may differ from a plain program's by a relative error of at most 0.0004.
Values may be sent and summed in bfloat16 or wider, within the bound.
A program may use at most 128 MiB of HBM per device.

v0:
```python
import jax
import jax.numpy as jnp
from jax import lax
from jax.sharding import Mesh
from jax.sharding import PartitionSpec as P

FSDP = ("fsdp_0", "fsdp_1")
FSDP_WIDTH = ("fsdp_0", "fsdp_1", "width")
learn_rate = 0.3
hold_rate = 0.9


def one_axis_at_a_time(array, axes):
    for axis in axes:
        array = lax.psum(array, axis)
    return array


def side_by_side(arrays, axis, dim, along):
    both = jnp.concatenate(arrays, axis=along)
    result, at, done = (lax.all_gather(both, axis, axis=dim, tiled=True), 0, [])
    for a in arrays:
        done.append(lax.slice_in_dim(result, at, at + a.shape[along], axis=along))
        at += a.shape[along]
    return tuple(done)


def shards(
    train_gate, drift_gate, spread_gate, train_up, drift_up, spread_up, norm_train, norm_step
):
    hold_gate = hold_rate * drift_gate + spread_gate
    whole_gate = train_gate - learn_rate * hold_gate
    hold_up = hold_rate * drift_up + spread_up
    whole_up = train_up - learn_rate * hold_up
    total_gate, total_up = (
        one_axis_at_a_time(jnp.sum(whole_gate * whole_gate, axis=0), FSDP),
        one_axis_at_a_time(jnp.sum(whole_up * whole_up, axis=0), FSDP),
    )
    scale_gate = jnp.sqrt(total_gate)
    scale_up = jnp.sqrt(total_up)
    narrow_gate, narrow_up = (
        (whole_gate / scale_gate).astype(jnp.bfloat16),
        (whole_up / scale_up).astype(jnp.bfloat16),
    )
    serving_gate, serving_up = side_by_side((narrow_gate, narrow_up), FSDP, 0, 1)
    serve_norm = lax.all_gather(
        (norm_train + norm_step).astype(jnp.bfloat16), FSDP_WIDTH, axis=0, tiled=True
    )
    return (serving_gate, serving_up, scale_gate, scale_up, serve_norm, whole_gate, whole_up)


def solution(mesh):
    split = Mesh(mesh.devices.reshape(4, 4, mesh.shape["width"]), ("fsdp_0", "fsdp_1", "width"))
    in_specs = (
        P(FSDP, "width"),
        P(FSDP, "width"),
        P(FSDP, "width"),
        P(FSDP, "width"),
        P(FSDP, "width"),
        P(FSDP, "width"),
        P(FSDP_WIDTH),
        P(FSDP_WIDTH),
    )
    out_specs = (
        P(None, "width"),
        P(None, "width"),
        P("width"),
        P("width"),
        P(),
        P(FSDP, "width"),
        P(FSDP, "width"),
    )
    return jax.shard_map(
        shards, mesh=split, in_specs=in_specs, out_specs=out_specs, check_vma=False
    )
```

profile of v0, /device:TPU:2, one launch (start us, length us, event | category | flops | bytes accessed | tf_op | source)
XLA Modules:
  0.0 145.8 jit_solution(3862906683493786616)
XLA Ops:
  7.2 0.0 copy-start.4
  7.2 0.0 copy-start.5
  7.2 0.0 all-gather.2.cloned.1.call-start
  7.2 2.5 %multiply_reduce_fusion = (f32[688]{0:T(1024)S(1)}, f32[256,688]{0,1:T(8,128)S(1)}, f32[688]{0:T(1024)S(1)}, f32[256,688]{0,1:T(8,128)S(1)}) fusion(f32[256,688]{0,1:T(8,128)} %param.11, f32[256,688]{0,1:T(8,128)} %param.13, f32[256,688]{0,1:T(8,128)} %param.12, f32[256,688]{0,1:T(8,128)} %param.8, f32[256,688]{0,1:T(8,128)} %param.10, f32[256,688]{0,1:T(8,128)} %param.9), kind=kLoop, calls=%fused_computation.2 | loop fusion | flops 2112160 | bytes 5641600 | tf_op jit(solution)/shard_map/reduce_sum | solution.py:37
  9.8 0.0 copy-start
  9.8 0.0 copy-start.1
  9.8 10.9 %all-reduce.2 = (f32[688]{0:T(1024)S(1)}, f32[688]{0:T(1024)S(1)}) all-reduce(f32[688]{0:T(1024)S(1)} %get-tuple-element.13, f32[688]{0:T(1024)S(1)} %get-tuple-element.17), channel_id=1, replica_groups=mesh['fsdp_0'=4,'fsdp_1'=4,'width'=16] {'fsdp_0'}, use_global_device_ids=true, to_apply=%region_4.0 | all-reduce | flops 1376 | bytes 11008 | tf_op jit(solution)/shard_map/psum | solution.py:15
  20.7 8.8 %all-reduce.1 = (f32[688]{0:T(1024)S(1)}, f32[688]{0:T(1024)S(1)}) all-reduce(f32[688]{0:T(1024)S(1)} %get-tuple-element.9, f32[688]{0:T(1024)S(1)} %get-tuple-element.10), channel_id=1, replica_groups=mesh['fsdp_0'=4,'fsdp_1'=4,'width'=16] {'fsdp_1'}, use_global_device_ids=true, to_apply=%region_5.0 | all-reduce | flops 1376 | bytes 11008 | tf_op jit(solution)/shard_map/psum | solution.py:15
  29.5 0.0 copy-start.2
  29.5 0.0 copy-start.3
  29.5 0.2 divide_convert_fusion.1
  29.7 0.2 divide_convert_fusion
  29.9 0.9 pad_maximum_fusion
  30.8 0.0 all-gather.2.cloned.1.call-update
  30.8 0.0 copy-done.4
  30.8 0.0 copy-done.5
  30.8 0.2 dynamic-update-slice
  31.1 80.0 %all-reduce = bf16[4096]{0:T(1024)(128)(2,1)} all-reduce(bf16[4096]{0:T(1024)(128)(2,1)S(1)} %dynamic-update-slice), channel_id=1, replica_groups=mesh['fsdp_0'=4,'fsdp_1'=4,'width'=16] {'fsdp_0','fsdp_1','width'}, use_global_device_ids=true, to_apply=%add | all-reduce | flops 4096 | bytes 16384
  111.0 17.4 %all-gather.2.cloned.1.call-done = bf16[4096,1376]{0,1:T(8,128)(2,1)} async-done(((bf16[256,1376]{0,1:T(8,128)(2,1)}), bf16[4096,1376]{0,1:T(8,128)(2,1)}) %all-gather.2.cloned.1.call-update) | async-done | bytes 11272208 | tf_op jit(solution)/shard_map/all_gather | solution.py:21
  128.5 10.5 %fusion = (bf16[4096,688]{0,1:T(8,128)(2,1)}, bf16[4096,688]{0,1:T(8,128)(2,1)}) fusion(bf16[4096,1376]{0,1:T(8,128)(2,1)} %all-gather.2.cloned.1.call-done), kind=kLoop, calls=%fused_computation.8 | loop fusion | bytes 22544384 | tf_op jit(solution)/shard_map/slice | solution.py:23
  138.9 0.0 copy-done
  138.9 0.0 copy-done.1
  138.9 0.0 copy-done.2
  138.9 0.0 copy-done.3
  (4 shorter events, 0.0 us)
Async XLA Ops:
  7.2 23.6 %copy-start.4 = (f32[16]{0:T(128)S(1)}, f32[16]{0:T(128)}, u32[]{:S(2)}) copy-start(f32[16]{0:T(128)} %param.14) | copy-start | bytes 196
  7.2 23.6 %copy-start.5 = (f32[16]{0:T(128)S(1)}, f32[16]{0:T(128)}, u32[]{:S(2)}) copy-start(f32[16]{0:T(128)} %param.15) | copy-start | bytes 196
  7.2 121.3 %all-gather.2.cloned.1.call-start = ((), (), s32[]{:S(2)}) async-start(), calls=%async_computation | async-start | bytes 11976704 | tf_op jit(solution)/shard_map/all_gather | solution.py:21
  9.8 129.2 %copy-start = (f32[256,688]{0,1:T(8,128)}, f32[256,688]{0,1:T(8,128)S(1)}, u32[]{:S(2)}) copy-start(f32[256,688]{0,1:T(8,128)S(1)} %get-tuple-element.14) | copy-start | bytes 2113540
  9.8 129.2 %copy-start.1 = (f32[256,688]{0,1:T(8,128)}, f32[256,688]{0,1:T(8,128)S(1)}, u32[]{:S(2)}) copy-start(f32[256,688]{0,1:T(8,128)S(1)} %get-tuple-element.18) | copy-start | bytes 2113540
  29.5 109.4 %copy-start.2 = (f32[688]{0:T(1024)}, f32[688]{0:T(1024)S(1)}, u32[]{:S(2)}) copy-start(f32[688]{0:T(1024)S(1)} %sqrt.6) | copy-start | bytes 8260
  29.5 109.4 %copy-start.3 = (f32[688]{0:T(1024)}, f32[688]{0:T(1024)S(1)}, u32[]{:S(2)}) copy-start(f32[688]{0:T(1024)S(1)} %sqrt.7) | copy-start | bytes 8260
Sparse Core Ops, SparseCore 0:
  30.9 97.5 all-gather.1
where the time goes:
time: 146 us
  blocking collectives  99.6 us (68%)
  waiting for transfers between devices  17.4 us (12%)
  between operations  14.2 us (10%)
  local copies, waits for them, and re-layouts  10.8 us (7%)
  other arithmetic  3.76 us (3%)
    unnamed x1, blocking collectives  80 us
    psum x2, blocking collectives, one_axis_at_a_time(): array = lax.psum(array, axis)  19.7 us
    all_gather x1, waiting for transfers between devices, side_by_side(): result, at, done = (lax.all_gather(both, axis, axis=dim, tiled=True), 0, [])  17.4 us
    slice x1, local copies, waits for them, and re-layouts, side_by_side(): done.append(lax.slice_in_dim(result, at, at + a.shape[along], axis=along))  10.5 us
  transfers between devices with their start and end apart: 1, of which 1 were waited for; matrix products, arithmetic and copies ran while one was open for 0% of the time, Pallas kernels for 0%

commit v1 on v0

--- a/solution.py
+++ b/solution.py
@@ -12,7 +12,7 @@
 
 def one_axis_at_a_time(array, axes):
     for axis in axes:
-        array = lax.psum(array, axis)
+        array = jnp.sum(lax.all_gather(array, axis), axis=0)
     return array
 
 

time: 146 us -> 166 us (1.14)
  blocking collectives: 99.6 us -> 112 us
  local copies, waits for them, and re-layouts: 10.8 us -> 14.1 us
    unnamed x1 -> x3, blocking collectives: 80 us -> 112 us
    psum x2 -> x0, blocking collectives: 19.7 us -> none  [one_axis_at_a_time(): array = lax.psum(array, axis)]
    unnamed x14 -> x26, local copies, waits for them, and re-layouts: 0.29 us -> 3.35 us
    reduce_sum x0 -> x5, other arithmetic: none -> 1.81 us  [the longest x1 1.75 us: shards(): jnp.sum(whole_gate * whole_gate, axis=0)]
where the time goes in v1:
time: 166 us; the launch traced here: 165 us
  blocking collectives  112 us (67%)
  waiting for transfers between devices  18.7 us (11%)
  between operations  15.5 us (9%)
  local copies, waits for them, and re-layouts  14.1 us (8%)
  other arithmetic  4.72 us (3%)
    unnamed x3, blocking collectives  112 us
    all_gather x1, waiting for transfers between devices, side_by_side(): result, at, done = (lax.all_gather(both, axis, axis=dim, tiled=True), 0, [])  18.7 us
    slice x1, local copies, waits for them, and re-layouts, side_by_side(): done.append(lax.slice_in_dim(result, at, at + a.shape[along], axis=along))  10.5 us
    unnamed x26, local copies, waits for them, and re-layouts  3.35 us
  transfers between devices with their start and end apart: 1, of which 1 were waited for; matrix products, arithmetic and copies ran while one was open for 0% of the time, Pallas kernels for 0%

profile of v1, /device:TPU:2, one launch (start us, length us, event | category | flops | bytes accessed | tf_op | source)
XLA Modules:
  0.0 165.4 jit_solution(9445772409569981354)
XLA Ops:
  7.2 0.0 copy-start.6
  7.2 0.0 copy-start.4
  7.2 0.0 copy-start.5
  7.2 0.0 all-gather.6.cloned.1.call-start
  7.2 1.3 dynamic-slice
  9.2 1.7 %multiply_reduce_fusion.1 = (f32[688]{0:T(1024)S(1)}, f32[256,688]{0,1:T(8,128)S(1)}) fusion(f32[256,688]{0,1:T(8,128)} %param.8, f32[256,688]{0,1:T(8,128)} %param.10, f32[256,688]{0,1:T(8,128)} %param.9), kind=kLoop, calls=%fused_computation.5 | loop fusion | flops 1056080 | bytes 2820800 | tf_op jit(solution)/shard_map/reduce_sum | solution.py:36
  10.9 0.0 copy-start
  10.9 0.3 dynamic-update-slice
  11.2 1.7 %multiply_reduce_fusion = (f32[688]{0:T(1024)S(1)}, f32[256,688]{0,1:T(8,128)S(1)}) fusion(f32[256,688]{0,1:T(8,128)} %param.11, f32[256,688]{0,1:T(8,128)} %param.13, f32[256,688]{0,1:T(8,128)} %param.12), kind=kLoop, calls=%fused_computation.2 | loop fusion | flops 1056080 | bytes 2820800 | tf_op jit(solution)/shard_map/reduce_sum | solution.py:37
  13.0 0.0 copy-start.1
  13.0 0.3 dynamic-update-slice.2
  13.3 17.2 %all-reduce.6 = (f32[2752]{0:T(1024)S(1)}, f32[2752]{0:T(1024)S(1)}) all-reduce(f32[2752]{0:T(1024)S(1)} %dynamic-update-slice.2, f32[2752]{0:T(1024)S(1)} %dynamic-update-slice), channel_id=4, replica_groups=mesh['fsdp_0'=4,'fsdp_1'=4,'width'=16] {'fsdp_0'}, use_global_device_ids=true, to_apply=%add.2 | all-reduce | flops 5504 | bytes 44032
  30.5 0.1 reshape.20
  30.6 0.0 copy-done.6
  30.6 0.6 dynamic-slice.1
  31.8 0.1 reshape.22
  31.9 0.3 dynamic-update-slice.1
  32.2 0.3 dynamic-update-slice.3
  32.5 14.0 %all-reduce.5 = (f32[2752]{0:T(1024)S(1)}, f32[2752]{0:T(1024)S(1)}) all-reduce(f32[2752]{0:T(1024)S(1)} %dynamic-update-slice.3, f32[2752]{0:T(1024)S(1)} %dynamic-update-slice.1), channel_id=5, replica_groups=mesh['fsdp_0'=4,'fsdp_1'=4,'width'=16] {'fsdp_1'}, use_global_device_ids=true, to_apply=%add.3 | all-reduce | flops 5504 | bytes 44032
  46.5 0.1 reshape.21
  46.6 0.0 copy-start.2
  46.6 0.1 reshape.23
  46.7 0.0 copy-start.3
  46.7 0.3 divide_convert_fusion
  47.0 0.9 pad_maximum_fusion
  47.9 0.0 all-gather.6.cloned.1.call-update
  47.9 0.0 copy-done.4
  47.9 0.0 copy-done.5
  48.0 0.2 dynamic-update-slice.4
  48.2 81.2 %all-reduce.4 = bf16[4096]{0:T(1024)(128)(2,1)} all-reduce(bf16[4096]{0:T(1024)(128)(2,1)S(1)} %dynamic-update-slice.4), channel_id=1, replica_groups=mesh['fsdp_0'=4,'fsdp_1'=4,'width'=16] {'fsdp_0','fsdp_1','width'}, use_global_device_ids=true, to_apply=%add.4 | all-reduce | flops 4096 | bytes 16384
  129.4 18.7 %all-gather.6.cloned.1.call-done = bf16[4096,1376]{0,1:T(8,128)(2,1)} async-done(((bf16[256,1376]{0,1:T(8,128)(2,1)}), bf16[4096,1376]{0,1:T(8,128)(2,1)}) %all-gather.6.cloned.1.call-update) | async-done | bytes 11272208 | tf_op jit(solution)/shard_map/all_gather | solution.py:21
  148.1 10.5 %fusion = (bf16[4096,688]{0,1:T(8,128)(2,1)}, bf16[4096,688]{0,1:T(8,128)(2,1)}) fusion(bf16[4096,1376]{0,1:T(8,128)(2,1)} %all-gather.6.cloned.1.call-done), kind=kLoop, calls=%fused_computation.8 | loop fusion | bytes 22544384 | tf_op jit(solution)/shard_map/slice | solution.py:23
  158.6 0.0 copy-done
  158.6 0.0 copy-done.1
  158.6 0.0 copy-done.2
  158.6 0.0 copy-done.3
  (12 shorter events, 0.1 us)
Async XLA Ops:
  7.2 23.4 %copy-start.6 = (u32[256]{0:T(256)S(1)}, u32[256]{0:T(256)}, u32[]{:S(2)}) copy-start(u32[256]{0:T(256)} %constant.15) | copy-start | bytes 3076
  7.2 40.8 %copy-start.4 = (f32[16]{0:T(128)S(1)}, f32[16]{0:T(128)}, u32[]{:S(2)}) copy-start(f32[16]{0:T(128)} %param.14) | copy-start | bytes 196
  7.2 40.8 %copy-start.5 = (f32[16]{0:T(128)S(1)}, f32[16]{0:T(128)}, u32[]{:S(2)}) copy-start(f32[16]{0:T(128)} %param.15) | copy-start | bytes 196
  7.2 140.9 %all-gather.6.cloned.1.call-start = ((), (), s32[]{:S(2)}) async-start(), calls=%async_computation | async-start | bytes 11976704 | tf_op jit(solution)/shard_map/all_gather | solution.py:21
  10.9 147.6 %copy-start = (f32[256,688]{0,1:T(8,128)}, f32[256,688]{0,1:T(8,128)S(1)}, u32[]{:S(2)}) copy-start(f32[256,688]{0,1:T(8,128)S(1)} %get-tuple-element.12) | copy-start | bytes 2113540
  13.0 145.6 %copy-start.1 = (f32[256,688]{0,1:T(8,128)}, f32[256,688]{0,1:T(8,128)S(1)}, u32[]{:S(2)}) copy-start(f32[256,688]{0,1:T(8,128)S(1)} %get-tuple-element.14) | copy-start | bytes 2113540
  46.6 112.0 %copy-start.2 = (f32[688]{0:T(1024)}, f32[688]{0:T(1024)S(1)}, u32[]{:S(2)}) copy-start(f32[688]{0:T(1024)S(1)} %sqrt.14) | copy-start | bytes 8260
  46.7 111.8 %copy-start.3 = (f32[688]{0:T(1024)}, f32[688]{0:T(1024)S(1)}, u32[]{:S(2)}) copy-start(f32[688]{0:T(1024)S(1)} %sqrt.15) | copy-start | bytes 8260
Sparse Core Ops, SparseCore 0:
  48.1 100.0 all-gather.5
